TPU v7x, 32 devices: a whole 2x2x4 slice. The times are simulated.
32 devices in a mesh: dp: 16 (over z, y, x), mp: 2 (over core).
Axes of the slice: x: 2, y: 2, z: 4, core: 2. Of those that a mesh axis runs over, the one named last changes fastest.
Arguments:
- tokens: bfloat16 [32768, 768], P(('dp', 'mp')), may hold values from -6 to 6
- w_query: bfloat16 [768, 768], P('dp', 'mp'), may hold values from -0.625 to 0.625
- w_key: bfloat16 [768, 768], P('dp', 'mp'), may hold values from -0.625 to 0.625
- w_value: bfloat16 [768, 768], P('dp', 'mp'), may hold values from -0.21875 to 0.21875
- value_taps: float32 [12, 33], P('mp'), may hold values from -0.3 to 0.3
- w_output: bfloat16 [768, 768], P(None, ('dp', 'mp')), may hold values from -0.875 to 0.875
- first_gain: bfloat16 [768], P(('dp', 'mp')), may hold values from 0.25 to 1.75
- first_bias: bfloat16 [768], P(('dp', 'mp')), may hold values from -1.5 to 1.5
- w_expand: bfloat16 [768, 3072], P('dp', 'mp'), may hold values from -0.21875 to 0.21875
- w_shrink: bfloat16 [3072, 768], P('mp', 'dp'), may hold values from -0.21875 to 0.21875
- second_gain: bfloat16 [768], P(('dp', 'mp')), may hold values from 0.25 to 1.75
- second_bias: bfloat16 [768], P(('dp', 'mp')), may hold values from -1.5 to 1.5
- doc_lengths: int32 [32], replicated, may hold values from 256 to 1024, as said below
- out_grad: bfloat16 [32768, 768], P(('dp', 'mp')), may hold values from -6 to 6
Outputs:
- layer_out: bfloat16 [32768, 768], P(('dp', 'mp'))
- tokens_grad: float32 [32768, 768], P(('dp', 'mp'))
- query_grad: float32 [768, 768], P('dp', 'mp')
- key_grad: float32 [768, 768], P('dp', 'mp')
- value_grad: float32 [768, 768], P('dp', 'mp')
- taps_grad: float32 [12, 33], P('mp')
- output_grad: float32 [768, 768], P(None, ('dp', 'mp'))
- first_gain_grad: float32 [768], P(('dp', 'mp'))
- first_bias_grad: float32 [768], P(('dp', 'mp'))
- expand_grad: float32 [768, 3072], P('dp', 'mp')
- shrink_grad: float32 [3072, 768], P('mp', 'dp')
- second_gain_grad: float32 [768], P(('dp', 'mp'))
- second_bias_grad: float32 [768], P(('dp', 'mp'))
Inputs may be any that keep to these rules, and one draw needn't show every extreme that they name: Document i occupies the first doc_lengths[i] positions of slot i of 1024 positions; the rest is padding. In every draw some document fills its whole slot.
All inputs are finite; a program needn't handle non-finite values.
Results may differ from a plain program's by a relative error of at most 0.018.
The roundings to bfloat16 on the way count: a program that leaves them out, or rounds other values in their place, can miss the bound.
Values may be sent and summed in bfloat16 or wider, within the bound.
A program may use at most 320 MiB of HBM per device.

v0:
```python
import jax
import jax.numpy as jnp
from jax import lax
from jax.sharding import PartitionSpec as P

HEAD_DIM = 64
LANDMARKS = 64
KERNEL = 33
PINV_STEPS = 6
HIGH = lax.Precision.HIGHEST


def ahead(left, right):
    return jnp.dot(left, right, preferred_element_type=jnp.float32)


def against(left, right):
    return lax.dot_general(
        left, right, (((1,), (1,)), ((), ())), preferred_element_type=jnp.float32
    )


def across(left, right):
    return lax.dot_general(
        left, right, (((0,), (0,)), ((), ())), preferred_element_type=jnp.float32
    )


def layer_norm(values, gain, bias):
    middle = jnp.mean(values, axis=-1, keepdims=True)
    centered = values - middle
    variance = jnp.mean(centered * centered, axis=-1, keepdims=True)
    return centered * lax.rsqrt(variance + 1e-05) * gain + bias


def exact_gelu(values):
    return jax.nn.gelu(values, approximate=False)


def inverse_estimate(matrix):
    widest = jnp.max(jnp.sum(matrix, axis=-2), axis=-1)
    current = jnp.swapaxes(matrix, -1, -2) / widest[:, None, None]
    identity = jnp.eye(matrix.shape[-1], dtype=jnp.float32)[None]
    for step in range(PINV_STEPS):
        product = jnp.einsum("hij,hjk->hik", matrix, current, precision=HIGH)
        inner_term = 7.0 * identity - product
        inner_term = 15.0 * identity - jnp.einsum(
            "hij,hjk->hik", product, inner_term, precision=HIGH
        )
        inner_term = 13.0 * identity - jnp.einsum(
            "hij,hjk->hik", product, inner_term, precision=HIGH
        )
        current = 0.25 * jnp.einsum("hij,hjk->hik", current, inner_term, precision=HIGH)
    return current


def nystrom(query, keys, values, taps, length):
    slots = query.shape[0]
    positions = jnp.arange(slots, dtype=jnp.int32)
    valid = positions < length
    weight = valid.astype(jnp.float32)
    segment = positions * LANDMARKS // length
    member = (
        (segment[None, :] == jnp.arange(LANDMARKS, dtype=jnp.int32)[:, None]) & valid[None, :]
    ).astype(jnp.float32)
    member = member / jnp.sum(member, axis=1, keepdims=True)
    mark_query = jnp.einsum("js,shd->hjd", member, query, precision=HIGH)
    mark_keys = jnp.einsum("js,shd->hjd", member, keys, precision=HIGH)
    scale = HEAD_DIM ** (-0.5)
    first = jax.nn.softmax(
        jnp.einsum("shd,hjd->hsj", query, mark_keys, precision=HIGH) * scale, axis=-1
    )
    second = jax.nn.softmax(
        jnp.einsum("hid,hjd->hij", mark_query, mark_keys, precision=HIGH) * scale, axis=-1
    )
    third_scores = jnp.einsum("hjd,shd->hjs", mark_query, keys, precision=HIGH) * scale
    third = jax.nn.softmax(jnp.where(valid[None, None, :], third_scores, -1e30), axis=-1)
    inverse = inverse_estimate(second)
    summary = jnp.einsum("hjs,shd->hjd", third, values, precision=HIGH)
    carried = jnp.einsum("hij,hjd->hid", inverse, summary, precision=HIGH)
    mixed = jnp.einsum("hsj,hjd->shd", first, carried, precision=HIGH)
    radius = KERNEL // 2
    padded = jnp.pad(values * weight[:, None, None], ((radius, radius), (0, 0), (0, 0)))
    for index in range(KERNEL):
        mixed = mixed + taps[:, index][None, :, None] * padded[index : index + slots]
    mixed = mixed * weight[:, None, None]
    return mixed.reshape(slots, query.shape[1] * HEAD_DIM)


def on_device(
    tokens,
    w_query,
    w_key,
    w_value,
    value_taps,
    w_output,
    first_gain,
    first_bias,
    w_expand,
    w_shrink,
    second_gain,
    second_bias,
    doc_lengths,
    out_grad,
):
    parts = lax.axis_size("mp")
    group = lax.axis_index("dp")
    slots = tokens.shape[0]
    pair = lax.dynamic_slice_in_dim(doc_lengths, group * parts, parts)
    full_query, full_keys, full_values, full_expand, full_shrink = (
        lax.all_gather(w_query, "dp", axis=0, tiled=True),
        lax.all_gather(w_key, "dp", axis=0, tiled=True),
        lax.all_gather(w_value, "dp", axis=0, tiled=True),
        lax.all_gather(w_expand, "dp", axis=0, tiled=True),
        lax.all_gather(w_shrink, "dp", axis=1, tiled=True),
    )
    full_output, gain_one, bias_one, gain_two, bias_two = (
        lax.all_gather(w_output, ("dp", "mp"), axis=1, tiled=True),
        lax.all_gather(first_gain, ("dp", "mp"), axis=0, tiled=True),
        lax.all_gather(first_bias, ("dp", "mp"), axis=0, tiled=True),
        lax.all_gather(second_gain, ("dp", "mp"), axis=0, tiled=True),
        lax.all_gather(second_bias, ("dp", "mp"), axis=0, tiled=True),
    )
    gain_one = gain_one.astype(jnp.float32)
    bias_one = bias_one.astype(jnp.float32)
    gain_two = gain_two.astype(jnp.float32)
    bias_two = bias_two.astype(jnp.float32)
    local_heads = full_query.shape[1] // HEAD_DIM
    grouped = lax.all_gather(tokens, "mp", axis=0, tiled=True)
    query_low = ahead(grouped, full_query).astype(jnp.bfloat16)
    keys_low = ahead(grouped, full_keys).astype(jnp.bfloat16)
    values_low = ahead(grouped, full_values).astype(jnp.bfloat16)

    def attention_core(query, keys, values, taps):
        shape = (parts, slots, local_heads, HEAD_DIM)
        mixed = jax.vmap(nystrom, in_axes=(0, 0, 0, None, 0))(
            query.reshape(shape), keys.reshape(shape), values.reshape(shape), taps, pair
        )
        return mixed.reshape(parts * slots, local_heads * HEAD_DIM)

    attended, core_back = jax.vjp(
        attention_core,
        query_low.astype(jnp.float32),
        keys_low.astype(jnp.float32),
        values_low.astype(jnp.float32),
        value_taps,
    )
    attended_tok = lax.all_to_all(
        attended.astype(jnp.bfloat16), "mp", split_axis=0, concat_axis=1, tiled=True
    )
    projected = ahead(attended_tok, full_output)
    first_out, first_back = jax.vjp(
        layer_norm, tokens.astype(jnp.float32) + projected, gain_one, bias_one
    )
    hidden_all = lax.all_gather(first_out.astype(jnp.bfloat16), "mp", axis=0, tiled=True)
    pre = ahead(hidden_all, full_expand)
    active, gelu_back = jax.vjp(exact_gelu, pre)
    active_low = active.astype(jnp.bfloat16)
    branch = lax.psum_scatter(
        ahead(active_low, full_shrink).astype(jnp.bfloat16), "mp", scatter_dimension=0, tiled=True
    ).astype(jnp.float32)
    result, second_back = jax.vjp(layer_norm, first_out + branch, gain_two, bias_two)
    layer_out = result.astype(jnp.bfloat16)
    d_second_in, gain_two_grad, bias_two_grad = second_back(out_grad.astype(jnp.float32))
    branch_grad = lax.all_gather(d_second_in.astype(jnp.bfloat16), "mp", axis=0, tiled=True)
    back_query, back_keys, back_values, back_expand, back_shrink = (
        lax.all_gather(w_query, "dp", axis=0, tiled=True),
        lax.all_gather(w_key, "dp", axis=0, tiled=True),
        lax.all_gather(w_value, "dp", axis=0, tiled=True),
        lax.all_gather(w_expand, "dp", axis=0, tiled=True),
        lax.all_gather(w_shrink, "dp", axis=1, tiled=True),
    )
    (d_pre,) = gelu_back(against(branch_grad, back_shrink))
    d_pre_low = d_pre.astype(jnp.bfloat16)
    shrink_grad = across(active_low, branch_grad)
    expand_grad = across(hidden_all, d_pre_low)
    d_hidden = lax.psum_scatter(
        against(d_pre_low, back_expand).astype(jnp.bfloat16), "mp", scatter_dimension=0, tiled=True
    ).astype(jnp.float32)
    d_first_in, gain_one_grad, bias_one_grad = first_back(d_second_in + d_hidden)
    d_projected = d_first_in.astype(jnp.bfloat16)
    output_grad = across(attended_tok, d_projected)
    d_attended = against(d_projected, full_output).astype(jnp.bfloat16)
    d_heads = lax.all_to_all(d_attended, "mp", split_axis=1, concat_axis=0, tiled=True)
    d_query, d_keys, d_values, taps_grad = core_back(d_heads.astype(jnp.float32))
    d_query = d_query.astype(jnp.bfloat16)
    d_keys = d_keys.astype(jnp.bfloat16)
    d_values = d_values.astype(jnp.bfloat16)
    query_grad = across(grouped, d_query)
    key_grad = across(grouped, d_keys)
    value_grad = across(grouped, d_values)
    total = against(d_query, back_query)
    total = total + against(d_keys, back_keys)
    tokens_grad = d_first_in + lax.psum_scatter(
        (total + against(d_values, back_values)).astype(jnp.bfloat16),
        "mp",
        scatter_dimension=0,
        tiled=True,
    ).astype(jnp.float32)
    query_grad, key_grad, value_grad, expand_grad, shrink_grad = (
        lax.psum_scatter(query_grad, "dp", scatter_dimension=0, tiled=True),
        lax.psum_scatter(key_grad, "dp", scatter_dimension=0, tiled=True),
        lax.psum_scatter(value_grad, "dp", scatter_dimension=0, tiled=True),
        lax.psum_scatter(expand_grad, "dp", scatter_dimension=0, tiled=True),
        lax.psum_scatter(shrink_grad, "dp", scatter_dimension=1, tiled=True),
    )
    output_grad, gain_one_grad, bias_one_grad, gain_two_grad, bias_two_grad = (
        lax.psum_scatter(output_grad, ("dp", "mp"), scatter_dimension=1, tiled=True),
        lax.psum_scatter(gain_one_grad, ("dp", "mp"), scatter_dimension=0, tiled=True),
        lax.psum_scatter(bias_one_grad, ("dp", "mp"), scatter_dimension=0, tiled=True),
        lax.psum_scatter(gain_two_grad, ("dp", "mp"), scatter_dimension=0, tiled=True),
        lax.psum_scatter(bias_two_grad, ("dp", "mp"), scatter_dimension=0, tiled=True),
    )
    taps_grad = lax.psum(taps_grad, "dp")
    return (
        layer_out,
        tokens_grad,
        query_grad,
        key_grad,
        value_grad,
        taps_grad,
        output_grad,
        gain_one_grad,
        bias_one_grad,
        expand_grad,
        shrink_grad,
        gain_two_grad,
        bias_two_grad,
    )


def solution(mesh):
    in_specs = (
        P(("dp", "mp"), None),
        P("dp", "mp"),
        P("dp", "mp"),
        P("dp", "mp"),
        P("mp", None),
        P(None, ("dp", "mp")),
        P(("dp", "mp")),
        P(("dp", "mp")),
        P("dp", "mp"),
        P("mp", "dp"),
        P(("dp", "mp")),
        P(("dp", "mp")),
        P(),
        P(("dp", "mp"), None),
    )
    out_specs = (
        P(("dp", "mp"), None),
        P(("dp", "mp"), None),
        P("dp", "mp"),
        P("dp", "mp"),
        P("dp", "mp"),
        P("mp", None),
        P(None, ("dp", "mp")),
        P(("dp", "mp")),
        P(("dp", "mp")),
        P("dp", "mp"),
        P("mp", "dp"),
        P(("dp", "mp")),
        P(("dp", "mp")),
    )
    return jax.shard_map(
        on_device, mesh=mesh, in_specs=in_specs, out_specs=out_specs, check_vma=False
    )
```

profile of v0, /device:TPU:0, one launch (start us, length us, event | category | flops | bytes accessed | tf_op | source)
XLA Modules:
  0.0 1484.3 jit_solution(6945524106746862283)
XLA Ops:
  18.9 42.1 %all-reduce.76 = (bf16[768]{0:T(1024)(128)(2,1)S(1)}, bf16[768]{0:T(1024)(128)(2,1)S(1)}, bf16[768]{0:T(1024)(128)(2,1)}, bf16[768]{0:T(1024)(128)(2,1)}) all-reduce(bf16[768]{0:T(1024)(128)(2,1)S(1)} %dynamic-update-slice.1, bf16[768]{0:T(1024)(128)(2,1)S(1)} %dynamic-update-slice, ...), channel_id=1, replica_groups=mesh['dp'=16,'mp'=2] {'dp','mp'}, use_global_device_ids=true, to_apply=%add.68 | all-reduce | flops 3072 | bytes 12288
  62.4 44.0 %all_gather.45 = bf16[768,384]{1,0:T(8,128)(2,1)S(1)} all-gather(bf16[48,384]{1,0:T(8,128)(2,1)S(1)} %copy-done.119), channel_id=1, replica_groups=mesh['dp'=16,'mp'=2] {'dp'}, dimensions={0}, use_global_device_ids=true | all-gather | bytes 626688 | tf_op jit(solution)/shard_map/all_gather | solution.py:111
  106.3 41.1 %all_gather.46 = bf16[768,384]{1,0:T(8,128)(2,1)S(1)} all-gather(bf16[48,384]{1,0:T(8,128)(2,1)S(1)} %copy-done.120), channel_id=1, replica_groups=mesh['dp'=16,'mp'=2] {'dp'}, dimensions={0}, use_global_device_ids=true | all-gather | bytes 626688 | tf_op jit(solution)/shard_map/all_gather | solution.py:112
  147.4 43.7 %all_gather.47 = bf16[768,384]{1,0:T(8,128)(2,1)} all-gather(bf16[48,384]{1,0:T(8,128)(2,1)S(1)} %copy-done.121), channel_id=1, replica_groups=mesh['dp'=16,'mp'=2] {'dp'}, dimensions={0}, use_global_device_ids=true | all-gather | bytes 626688 | tf_op jit(solution)/shard_map/all_gather | solution.py:113
  191.8 4.8 convolution_convert_fusion.3
  200.9 4.8 convolution_convert_fusion.4
  217.6 3.9 multiply_reduce_fusion.39
  227.1 4.0 reshape.597
  261.4 4.2 reshape.598
  267.9 29.7 %multiply_convert_fusion.1 = bf16[2,1024,6,64]{1,3,2,0:T(8,128)(2,1)} fusion(f32[2,1024,6,64]{1,3,2,0:T(8,128)S(1)} %copy_multiply_fusion, f32[2,6,64,64]{3,2,1,0:T(8,128)S(1)} %fusion.157, f32[6]{0:T(128)S(1)} %copy-done.146, f32[6]{0:T(128)S(1)} %copy-done.156, f32[6]{0:T(128)S(1)} %copy-done.158, f32[6]{0:T(128)S(1)} %copy-done.160, ...), kind=kOutput, calls=%fused_computation.121 | convolution fusion | flops 659816448 | bytes 8168216 | tf_op jit(solution)/shard_map/jvp(vmap(hsj,hjd->shd))/dot_general | solution.py:81
  297.5 3.7 all-to-all-start
  311.6 7.5 all-gather.11.cloned.1.call-done
  319.1 35.5 %multiply_convert_fusion = (bf16[2048,1536]{1,0:T(8,128)(2,1)}, f32[2048,1536]{1,0:T(8,128)}, f32[2048,1536]{1,0:T(8,128)}) fusion(bf16[2048,768]{0,1:T(8,128)(2,1)} %all-gather.11.cloned.1.call-done, bf16[768,1536]{1,0:T(8,128)(2,1)} %all-gather.13.cloned.1.call-done), kind=kOutput, calls=%fused_computation.3 | convolution fusion | flops 5036310528 | bytes 36962304 | tf_op jit(solution)/shard_map/dot_general | solution.py:14
  354.6 30.5 %all-gather.15.cloned.1.call-done = bf16[1536,768]{0,1:T(8,128)(2,1)} async-done(((bf16[1536,48]{0,1:T(8,128)(2,1)}), bf16[1536,768]{0,1:T(8,128)(2,1)}) %all-gather.15.cloned.1.call-update) | async-done | bytes 2359312 | tf_op jit(solution)/shard_map/all_gather | solution.py:115
  385.1 9.1 convolution_convert_fusion.1
  397.4 6.2 reduce-scatter.16.cloned.1.call-done
  415.1 13.5 all-gather.17.cloned.1.call-done
  428.6 17.3 %add_convert_fusion = bf16[2048,1536]{1,0:T(8,128)(2,1)S(1)} fusion(f32[2048,1536]{1,0:T(8,128)} %get-tuple-element.153, f32[2048,1536]{1,0:T(8,128)} %get-tuple-element.200, bf16[2048,768]{0,1:T(8,128)(2,1)} %all-gather.17.cloned.1.call-done, bf16[1536,768]{0,1:T(8,128)(2,1)} %all-gather.15.cloned.1.call-done), kind=kOutput, calls=%fused_computation.2 | convolution fusion | flops 4875878400 | bytes 36962304 | tf_op jit(solution)/shard_map/dot_general | solution.py:18
  448.6 6.4 convolution_convert_fusion
  459.4 8.0 reduce-scatter.18.cloned.1.call-done
  467.4 4.5 multiply_reduce_fusion
  475.5 5.0 all_to_all.29
  486.2 5.6 fusion.15
  534.2 15.2 %multiply_reduce_fusion.32 = (f32[6]{0:T(128)}, f32[6]{0:T(128)}, f32[6]{0:T(128)}, f32[6]{0:T(128)}, f32[6]{0:T(128)}, /*index=5*/f32[6]{0:T(128)}, f32[6]{0:T(...) fusion(f32[2,1024,6,64]{1,3,2,0:T(8,128)S(1)} %copy-done.5, ...), kind=kLoop, calls=%fused_computation.107 | loop fusion | flops 25952166 | bytes 12591512 | tf_op jit(solution)/shard_map/transpose(jvp(vmap()))/reduce_sum | solution.py:85
  549.6 16.9 %broadcast_multiply_fusion.1 = (f32[2,1024,6,64]{1,3,2,0:T(8,128)}, f32[2,1024,6,64]{1,3,2,0:T(8,128)}, f32[2,1024,6,64]{1,3,2,0:T(8,128)}, f32[2,1024,6,64]{1,3...) fusion(f32[6]{0:T(128)S(1)} %copy-done.157, ...), kind=kLoop, calls=%fused_computation.168 | loop fusion | flops 11796480 | bytes 47194448 | tf_op jit(solution)/shard_map/transpose(jvp(vmap()))/mul | solution.py:85
  566.5 21.3 %broadcast_multiply_fusion = (f32[2,1024,6,64]{1,3,2,0:T(8,128)}, f32[2,1024,6,64]{1,3,2,0:T(8,128)}, f32[2,1024,6,64]{1,3,2,0:T(8,128)}, f32[2,1024,6,64]{1,3,2...) fusion(f32[6]{0:T(128)} %get-tuple-element.134, ...), kind=kLoop, calls=%fused_computation.167 | loop fusion | flops 14155776 | bytes 56631704 | tf_op jit(solution)/shard_map/transpose(jvp(vmap()))/mul | solution.py:85
  587.9 4.9 multiply_reduce_fusion.34
  592.9 4.3 fusion.143
  600.9 3.8 multiply_reduce_fusion.35
  604.8 3.9 fusion.142
  621.7 4.4 fusion.174
  626.1 4.4 fusion.173
  630.5 34.7 %pad_add_fusion = f32[2,1056,6,64]{1,3,2,0:T(8,128)} fusion(f32[2,1024,6,64]{1,3,2,0:T(8,128)} %get-tuple-element.163, f32[2,1024,6,64]{1,3,2,0:T(8,128)} %get-tuple-element.164, f32[2,1024,6,64]{1,3,2,0:T(8,128)} %get-tuple-element.165, f32[2,1024,6,64]{1,3,2,0:T(8,128)} %get-tuple-element.166, f32[2,1024,6,64]{1,3,2,0:T(8,128)} %get-tuple-element.167, ...), kind=kLoop, calls=%fused_computation.25 | loop fusion | flops 21086208 | bytes 88178688 | tf_op jit(solution)/shard_map/transpose(jvp(vmap()))/add_any | solution.py:85
  665.2 12.1 fusion.12
  684.2 4.8 convolution_bitcast_fusion.2
  691.7 5.0 convolution_bitcast_fusion.1
  699.4 4.8 convolution_bitcast_fusion
  706.9 5.2 fusion.74
  712.2 9.6 fusion.175
  721.8 9.7 fusion.172
  734.2 40.9 %all-reduce.75 = (f32[768]{0:T(1024)S(1)}, f32[768]{0:T(1024)S(1)}, f32[768]{0:T(1024)S(1)}, f32[768]{0:T(1024)S(1)}) all-reduce(f32[768]{0:T(1024)S(1)} %copy-done.126, f32[768]{0:T(1024)S(1)} %copy-done.127, f32[768]{0:T(1024)S(1)} %copy-done.124, f32[768]{0:T(1024)S(1)} %copy-done.125), channel_id=9, replica_groups=mesh['dp'=16,'mp'=2] {'dp','mp'}, use_global_device_ids=true, to_apply=%region_65.66.clone | all-reduce | flops 3072 | bytes 24576
  780.4 28.5 %multiply_reduce_fusion.33 = (f32[6]{0:T(128)S(1)}, f32[6]{0:T(128)S(1)}, f32[6]{0:T(128)S(1)}, f32[6]{0:T(128)S(1)}, f32[6]{0:T(128)S(1)}, /*index=5*/f32[6]{0:...) fusion(f32[2,1024,6,64]{1,3,2,0:T(8,128)} %copy-done.4, ...), kind=kLoop, calls=%fused_computation.108 | loop fusion | flops 27525018 | bytes 6300056 | tf_op jit(solution)/shard_map/transpose(jvp(vmap()))/reduce_sum | solution.py:85
  809.1 75.8 %psum.7 = f32[6,33]{0,1:T(8,128)S(1)} all-reduce(f32[6,33]{0,1:T(8,128)S(1)} %pad_add_fusion.7), channel_id=1, replica_groups=mesh['dp'=16,'mp'=2] {'dp'}, use_global_device_ids=true, to_apply=%region_62.63 | all-reduce | flops 198 | bytes 1584 | tf_op jit(solution)/shard_map/psum | solution.py:214
  890.8 66.8 %reduce-scatter.30.cloned.1.call-done = f32[48,384]{1,0:T(8,128)} async-done(((f32[768,384]{1,0:T(8,128)}), f32[48,384]{1,0:T(8,128)}) %reduce-scatter.30.cloned.1.call-update) | async-done | bytes 73744
  957.6 129.3 %reduce-scatter.32.cloned.1.call-done = f32[48,384]{1,0:T(8,128)} async-done(((f32[768,384]{1,0:T(8,128)}), f32[48,384]{1,0:T(8,128)}) %reduce-scatter.32.cloned.1.call-update) | async-done | bytes 73744
  1086.9 104.5 %reduce-scatter.22.cloned.1.call-done = f32[768,24]{0,1:T(8,128)} async-done(((f32[768,768]{0,1:T(8,128)}), f32[768,24]{0,1:T(8,128)}) %reduce-scatter.22.cloned.1.call-update) | async-done | bytes 73744 | tf_op jit(solution)/shard_map/reduce_scatter | solution.py:208
  1191.3 143.0 %reduce-scatter.26.cloned.1.call-done = f32[1536,48]{0,1:T(8,128)} async-done(((f32[1536,768]{0,1:T(8,128)}), f32[1536,48]{0,1:T(8,128)}) %reduce-scatter.26.cloned.1.call-update) | async-done | bytes 294928 | tf_op jit(solution)/shard_map/reduce_scatter | solution.py:205
  1334.3 143.3 %reduce-scatter.24.cloned.1.call-done = f32[48,1536]{1,0:T(8,128)} async-done(((f32[768,1536]{1,0:T(8,128)}), f32[48,1536]{1,0:T(8,128)}) %reduce-scatter.24.cloned.1.call-update) | async-done | bytes 294928 | tf_op jit(solution)/shard_map/reduce_scatter | solution.py:204
  (651 shorter events, 194.2 us)
Async XLA Ops:
  7.2 55.0 %copy-start.204 = (s32[32]{0:T(128)S(1)}, s32[32]{0:T(128)}, u32[]{:S(2)}) copy-start(s32[32]{0:T(128)} %param.26) | copy-start | bytes 388
  7.2 55.1 %copy-start.119 = (bf16[48,384]{1,0:T(8,128)(2,1)S(1)}, bf16[48,384]{1,0:T(8,128)(2,1)}, u32[]{:S(2)}) copy-start(bf16[48,384]{1,0:T(8,128)(2,1)} %param.15) | copy-start | bytes 110596
  7.2 99.1 %copy-start.120 = (bf16[48,384]{1,0:T(8,128)(2,1)S(1)}, bf16[48,384]{1,0:T(8,128)(2,1)}, u32[]{:S(2)}) copy-start(bf16[48,384]{1,0:T(8,128)(2,1)} %param.16) | copy-start | bytes 110596
  7.3 140.2 %copy-start.121 = (bf16[48,384]{1,0:T(8,128)(2,1)S(1)}, bf16[48,384]{1,0:T(8,128)(2,1)}, u32[]{:S(2)}) copy-start(bf16[48,384]{1,0:T(8,128)(2,1)} %param.17) | copy-start | bytes 110596
  7.3 184.5 %all-gather.7.cloned.1.call-start = ((), (), s32[]{:S(2)}) async-start(), calls=%async_computation.11 | async-start | bytes 4718592 | tf_op jit(solution)/shard_map/all_gather | solution.py:129
  8.0 293.3 %all-gather.9.cloned.1.call-start = ((), (), s32[]{:S(2)}) async-start(), calls=%async_computation.12 | async-start | bytes 1216512 | tf_op jit(solution)/shard_map/all_gather | solution.py:118
  8.7 302.8 %all-gather.13.cloned.1.call-start = ((), (), s32[]{:S(2)}) async-start(), calls=%async_computation.14 | async-start | bytes 2506752 | tf_op jit(solution)/shard_map/all_gather | solution.py:114
  62.3 151.3 %copy-start.102 = (pred[2,1024]{1,0:T(4,128)(4,1)}, pred[2,1024]{1,0:T(4,128)(4,1)S(1)}, u32[]{:S(2)}) copy-start(pred[2,1024]{1,0:T(4,128)(4,1)S(1)} %get-tuple-element.190) | copy-start | bytes 6148
  62.4 204.7 %copy-start.94 = (f32[2,1024]{1,0:T(2,128)}, f32[2,1024]{1,0:T(2,128)S(1)}, u32[]{:S(2)}) copy-start(f32[2,1024]{1,0:T(2,128)S(1)} %get-tuple-element.191) | copy-start | bytes 24580
  106.3 94.6 %copy-start.75 = (bf16[768,384]{1,0:T(8,128)(2,1)}, bf16[768,384]{1,0:T(8,128)(2,1)S(1)}, u32[]{:S(2)}) copy-start(bf16[768,384]{1,0:T(8,128)(2,1)S(1)} %all_gather.45) | copy-start | bytes 1769476
  147.4 44.4 %copy-start.77 = (bf16[768,384]{1,0:T(8,128)(2,1)}, bf16[768,384]{1,0:T(8,128)(2,1)S(1)}, u32[]{:S(2)}) copy-start(bf16[768,384]{1,0:T(8,128)(2,1)S(1)} %all_gather.46) | copy-start | bytes 1769476
  191.6 20.5 %copy-start.109 = (s32[2,1024]{1,0:T(2,128)}, s32[2,1024]{1,0:T(2,128)S(1)}, u32[]{:S(2)}) copy-start(s32[2,1024]{1,0:T(2,128)S(1)} %and_select_fusion) | copy-start | bytes 24580
  191.8 20.4 %copy-start.128 = (f32[2,64]{1,0:T(2,128)}, f32[2,64]{1,0:T(2,128)S(1)}, u32[]{:S(2)}) copy-start(f32[2,64]{1,0:T(2,128)S(1)} %convert_reduce_fusion.1) | copy-start | bytes 1540
  216.1 38.6 %copy-start = (f32[2,6,64,1024]{3,2,1,0:T(8,128)}, f32[2,6,64,1024]{3,2,1,0:T(8,128)S(1)}, u32[]{:S(2)}) copy-start(f32[2,6,64,1024]{3,2,1,0:T(8,128)S(1)} %get-tuple-element.195) | copy-start | bytes 9437188
  232.5 18.6 %copy-start.9 = (f32[2,6,64,64]{2,3,1,0:T(8,128)}, f32[2,6,64,64]{2,3,1,0:T(8,128)S(1)}, u32[]{:S(2)}) copy-start(f32[2,6,64,64]{2,3,1,0:T(8,128)S(1)} %get-tuple-element.193) | copy-start | bytes 589828
  232.5 18.6 %copy-start.100 = (f32[2,6,64]{2,1,0:T(8,128)}, f32[2,6,64]{2,1,0:T(8,128)S(1)}, u32[]{:S(2)}) copy-start(f32[2,6,64]{2,1,0:T(8,128)S(1)} %get-tuple-element.192) | copy-start | bytes 9220
  267.0 30.5 %copy-start.4 = (f32[2,1024,6,64]{1,3,2,0:T(8,128)}, f32[2,1024,6,64]{1,3,2,0:T(8,128)S(1)}, u32[]{:S(2)}) copy-start(f32[2,1024,6,64]{1,3,2,0:T(8,128)S(1)} %copy_multiply_fusion) | copy-start | bytes 9437188
  297.5 6.2 all-to-all-start
  301.2 17.8 %all-gather.11.cloned.1.call-start = ((), (), s32[]{:S(2)}) async-start(), calls=%async_computation.13 | async-start | bytes 4718592 | tf_op jit(solution)/shard_map/all_gather | solution.py:155
  310.9 74.2 %all-gather.15.cloned.1.call-start = ((), (), s32[]{:S(2)}) async-start(), calls=%async_computation.15 | async-start | bytes 2506752 | tf_op jit(solution)/shard_map/all_gather | solution.py:115
  311.5 92.2 %reduce-scatter.16.cloned.1.call-start = ((), (), s32[]{:S(2)}) async-start(), calls=%async_computation.16 | async-start | bytes 4718592 | tf_op jit(solution)/shard_map/reduce_scatter | solution.py:159
  394.2 34.4 %all-gather.17.cloned.1.call-start = ((), (), s32[]{:S(2)}) async-start(), calls=%async_computation.17 | async-start | bytes 4718592 | tf_op jit(solution)/shard_map/all_gather | solution.py:165
  415.1 52.3 %reduce-scatter.18.cloned.1.call-start = ((), (), s32[]{:S(2)}) async-start(), calls=%async_computation.18 | async-start | bytes 4718592 | tf_op jit(solution)/shard_map/reduce_scatter | solution.py:177
  428.6 20.0 %copy-start.206 = (bf16[768,1536]{1,0:T(8,128)(2,1)S(1)}, bf16[768,1536]{1,0:T(8,128)(2,1)}, u32[]{:S(2)}) copy-start(bf16[768,1536]{1,0:T(8,128)(2,1)} %all-gather.13.cloned.1.call-done) | copy-start | bytes 7077892
  455.1 430.5 %reduce-scatter.20.cloned.1.call-start = ((), (), s32[]{:S(2)}) async-start(), calls=%async_computation.19 | async-start | bytes 4718592 | tf_op jit(solution)/shard_map/reduce_scatter | solution.py:194
  549.6 16.9 %copy-start.137 = (f32[6]{0:T(128)S(1)}, f32[6]{0:T(128)}, u32[]{:S(2)}) copy-start(f32[6]{0:T(128)} %get-tuple-element.123) | copy-start | bytes 76
  566.5 21.3 %copy-start.104 = (pred[2,1024]{1,0:T(4,128)(4,1)S(1)}, pred[2,1024]{1,0:T(4,128)(4,1)}, u32[]{:S(2)}) copy-start(pred[2,1024]{1,0:T(4,128)(4,1)} %copy-done.102) | copy-start | bytes 6148
  684.1 206.7 %reduce-scatter.28.cloned.1.call-start = ((), (), s32[]{:S(2)}) async-start(), calls=%async_computation.23 | async-start | bytes 1253376
  691.6 266.0 %reduce-scatter.30.cloned.1.call-start = ((), (), s32[]{:S(2)}) async-start(), calls=%async_computation.24 | async-start | bytes 1253376
  699.4 387.5 %reduce-scatter.32.cloned.1.call-start = ((), (), s32[]{:S(2)}) async-start(), calls=%async_computation.25 | async-start | bytes 1253376
  706.9 484.5 %reduce-scatter.22.cloned.1.call-start = ((), (), s32[]{:S(2)}) async-start(), calls=%async_computation.20 | async-start | bytes 2433024 | tf_op jit(solution)/shard_map/reduce_scatter | solution.py:208
  712.1 622.2 %reduce-scatter.26.cloned.1.call-start = ((), (), s32[]{:S(2)}) async-start(), calls=%async_computation.22 | async-start | bytes 5013504 | tf_op jit(solution)/shard_map/reduce_scatter | solution.py:205
  721.8 755.8 %reduce-scatter.24.cloned.1.call-start = ((), (), s32[]{:S(2)}) async-start(), calls=%async_computation.21 | async-start | bytes 5013504 | tf_op jit(solution)/shard_map/reduce_scatter | solution.py:204
  780.3 28.6 %copy-start.186 = (f32[6]{0:T(128)S(1)}, f32[6]{0:T(128)}, u32[]{:S(2)}) copy-start(f32[6]{0:T(128)} %get-tuple-element.84) | copy-start | bytes 76
  780.3 28.6 %copy-start.187 = (f32[6]{0:T(128)S(1)}, f32[6]{0:T(128)}, u32[]{:S(2)}) copy-start(f32[6]{0:T(128)} %get-tuple-element.85) | copy-start | bytes 76
  780.3 28.6 %copy-start.188 = (f32[6]{0:T(128)S(1)}, f32[6]{0:T(128)}, u32[]{:S(2)}) copy-start(f32[6]{0:T(128)} %get-tuple-element.86) | copy-start | bytes 76
  780.3 28.6 %copy-start.189 = (f32[6]{0:T(128)S(1)}, f32[6]{0:T(128)}, u32[]{:S(2)}) copy-start(f32[6]{0:T(128)} %get-tuple-element.87) | copy-start | bytes 76
  780.3 28.6 %copy-start.190 = (f32[6]{0:T(128)S(1)}, f32[6]{0:T(128)}, u32[]{:S(2)}) copy-start(f32[6]{0:T(128)} %get-tuple-element.88) | copy-start | bytes 76
  780.3 28.6 %copy-start.191 = (f32[6]{0:T(128)S(1)}, f32[6]{0:T(128)}, u32[]{:S(2)}) copy-start(f32[6]{0:T(128)} %get-tuple-element.89) | copy-start | bytes 76
  780.3 28.6 %copy-start.192 = (f32[6]{0:T(128)S(1)}, f32[6]{0:T(128)}, u32[]{:S(2)}) copy-start(f32[6]{0:T(128)} %get-tuple-element.90) | copy-start | bytes 76
  780.3 28.6 %copy-start.193 = (f32[6]{0:T(128)S(1)}, f32[6]{0:T(128)}, u32[]{:S(2)}) copy-start(f32[6]{0:T(128)} %get-tuple-element.91) | copy-start | bytes 76
  780.3 28.6 %copy-start.194 = (f32[6]{0:T(128)S(1)}, f32[6]{0:T(128)}, u32[]{:S(2)}) copy-start(f32[6]{0:T(128)} %get-tuple-element.92) | copy-start | bytes 76
  780.3 28.6 %copy-start.195 = (f32[6]{0:T(128)S(1)}, f32[6]{0:T(128)}, u32[]{:S(2)}) copy-start(f32[6]{0:T(128)} %get-tuple-element.93) | copy-start | bytes 76
  780.3 28.6 %copy-start.196 = (f32[6]{0:T(128)S(1)}, f32[6]{0:T(128)}, u32[]{:S(2)}) copy-start(f32[6]{0:T(128)} %get-tuple-element.94) | copy-start | bytes 76
  780.4 28.6 %copy-start.197 = (f32[6]{0:T(128)S(1)}, f32[6]{0:T(128)}, u32[]{:S(2)}) copy-start(f32[6]{0:T(128)} %get-tuple-element.95) | copy-start | bytes 76
  780.4 28.6 %copy-start.198 = (f32[6]{0:T(128)S(1)}, f32[6]{0:T(128)}, u32[]{:S(2)}) copy-start(f32[6]{0:T(128)} %get-tuple-element.96) | copy-start | bytes 76
  780.4 28.6 %copy-start.199 = (f32[6]{0:T(128)S(1)}, f32[6]{0:T(128)}, u32[]{:S(2)}) copy-start(f32[6]{0:T(128)} %get-tuple-element.97) | copy-start | bytes 76
  780.4 28.6 %copy-start.200 = (f32[6]{0:T(128)S(1)}, f32[6]{0:T(128)}, u32[]{:S(2)}) copy-start(f32[6]{0:T(128)} %get-tuple-element.98) | copy-start | bytes 76
  (187 other events, 798.0 us)
Sparse Core Ops, SparseCore 0:
  9.6 14.8 all-gather.6
  27.4 56.4 all-gather.8
  86.7 69.3 all-gather.12
  311.0 8.0 all-gather.10
  321.7 63.3 all-gather.14
  394.3 9.3 reduce-scatter.15
  415.2 13.3 all-gather.16
  455.2 12.1 reduce-scatter.17
  684.2 12.2 reduce-scatter.19
  701.7 126.3 reduce-scatter.27
  833.4 124.1 reduce-scatter.29
  962.8 124.0 reduce-scatter.31
  1092.7 98.5 reduce-scatter.21
  1196.9 137.3 reduce-scatter.25
  1339.9 137.6 reduce-scatter.23
where the time goes:
time: 1490 us; the launch traced here: 1480 us
  waiting for transfers between devices  658 us (44%)
  blocking collectives  293 us (20%)
  matrix products  288 us (19%)
  other arithmetic  154 us (10%)
  local copies, waits for them, and re-layouts  70.2 us (5%)
  between operations  17.8 us (1%)
    unnamed x18, waiting for transfers between devices  199 us
    reduce_scatter x1, waiting for transfers between devices, on_device(): lax.psum_scatter(expand_grad, 'dp', scatter_dimension=0, tiled=True)  143 us
    reduce_scatter x1, waiting for transfers between devices, on_device(): lax.psum_scatter(shrink_grad, 'dp', scatter_dimension=1, tiled=True)  143 us
    reduce_scatter x1, waiting for transfers between devices, on_device(): lax.psum_scatter(output_grad, ('dp', 'mp'), scatter_dimension=1, tiled=True)  104 us
    unnamed x2, blocking collectives  83 us
    psum x1, blocking collectives, on_device(): taps_grad = lax.psum(taps_grad, 'dp')  75.8 us
    dot_general x6, matrix products, ahead(): return jnp.dot(left, right, preferred_element_type=jnp.float32)  60.9 us
    reduce_sum x4, other arithmetic, nystrom(): mixed = mixed + taps[:, index][None, :, None] * padded[index:index + slots]  46.4 us
  transfers between devices with their start and end apart: 16, of which 11 were waited for; matrix products, arithmetic and copies ran while one was open for 17% of the time, Pallas kernels for 0%

commit v1 on v0

--- a/solution.py
+++ b/solution.py
@@ -211,7 +211,11 @@
         lax.psum_scatter(gain_two_grad, ("dp", "mp"), scatter_dimension=0, tiled=True),
         lax.psum_scatter(bias_two_grad, ("dp", "mp"), scatter_dimension=0, tiled=True),
     )
-    taps_grad = lax.psum(taps_grad, "dp")
+    size, result_2 = (lax.axis_size("dp"), taps_grad)
+    for far in [1 << k for k in range(size.bit_length() - 1)]:
+        route = [(i, i ^ far) for i in range(size)]
+        result_2 = result_2 + lax.ppermute(result_2, "dp", route)
+    taps_grad = result_2
     return (
         layer_out,
         tokens_grad,

time: 1490 us -> 1490 us (level)
  blocking collectives: 293 us -> 216 us
  waiting for transfers between devices: 658 us -> 726 us
    psum x1 -> x0, blocking collectives: 75.8 us -> none  [on_device(): taps_grad = lax.psum(taps_grad, 'dp')]
    unnamed x18, waiting for transfers between devices: 199 us -> 263 us
    unnamed x461 -> x457, local copies, waits for them, and re-layouts: 37.1 us -> 37.2 us
  transfers between devices with their start and end apart: 16 -> 20, of which waited for: 11 -> 14; matrix products, arithmetic and copies ran while one was open for 17% -> 17% of each run, Pallas kernels for 0% -> 0%
where the time goes in v1:
time: 1490 us; the launch traced here: 1480 us
  waiting for transfers between devices  726 us (49%)
  matrix products  288 us (19%)
  blocking collectives  216 us (14%)
  other arithmetic  154 us (10%)
  local copies, waits for them, and re-layouts  70.3 us (5%)
  between operations  17.8 us (1%)
    unnamed x18, waiting for transfers between devices  263 us
    reduce_scatter x1, waiting for transfers between devices, on_device(): lax.psum_scatter(expand_grad, 'dp', scatter_dimension=0, tiled=True)  143 us
    reduce_scatter x1, waiting for transfers between devices, on_device(): lax.psum_scatter(shrink_grad, 'dp', scatter_dimension=1, tiled=True)  143 us
    reduce_scatter x1, waiting for transfers between devices, on_device(): lax.psum_scatter(output_grad, ('dp', 'mp'), scatter_dimension=1, tiled=True)  104 us
    unnamed x2, blocking collectives  82.2 us
    dot_general x6, matrix products, ahead(): return jnp.dot(left, right, preferred_element_type=jnp.float32)  60.8 us
    reduce_sum x4, other arithmetic, nystrom(): mixed = mixed + taps[:, index][None, :, None] * padded[index:index + slots]  46.4 us
    all_gather x1, blocking collectives, on_device(): lax.all_gather(w_query, 'dp', axis=0, tiled=True)  44 us
  transfers between devices with their start and end apart: 20, of which 14 were waited for; matrix products, arithmetic and copies ran while one was open for 17% of the time, Pallas kernels for 0%

profile of v1, /device:TPU:0, one launch (start us, length us, event | category | flops | bytes accessed | tf_op | source)
XLA Modules:
  0.0 1484.3 jit_solution(14730702727978279022)
XLA Ops:
  18.9 42.1 %all-reduce.76 = (bf16[768]{0:T(1024)(128)(2,1)S(1)}, bf16[768]{0:T(1024)(128)(2,1)S(1)}, bf16[768]{0:T(1024)(128)(2,1)}, bf16[768]{0:T(1024)(128)(2,1)}) all-reduce(bf16[768]{0:T(1024)(128)(2,1)S(1)} %dynamic-update-slice.1, bf16[768]{0:T(1024)(128)(2,1)S(1)} %dynamic-update-slice, ...), channel_id=1, replica_groups=mesh['dp'=16,'mp'=2] {'dp','mp'}, use_global_device_ids=true, to_apply=%add.68 | all-reduce | flops 3072 | bytes 12288
  62.4 44.0 %all_gather.45 = bf16[768,384]{1,0:T(8,128)(2,1)S(1)} all-gather(bf16[48,384]{1,0:T(8,128)(2,1)S(1)} %copy-done.119), channel_id=1, replica_groups=mesh['dp'=16,'mp'=2] {'dp'}, dimensions={0}, use_global_device_ids=true | all-gather | bytes 626688 | tf_op jit(solution)/shard_map/all_gather | solution.py:111
  106.4 41.2 %all_gather.46 = bf16[768,384]{1,0:T(8,128)(2,1)S(1)} all-gather(bf16[48,384]{1,0:T(8,128)(2,1)S(1)} %copy-done.120), channel_id=1, replica_groups=mesh['dp'=16,'mp'=2] {'dp'}, dimensions={0}, use_global_device_ids=true | all-gather | bytes 626688 | tf_op jit(solution)/shard_map/all_gather | solution.py:112
  147.6 43.8 %all_gather.47 = bf16[768,384]{1,0:T(8,128)(2,1)} all-gather(bf16[48,384]{1,0:T(8,128)(2,1)S(1)} %copy-done.121), channel_id=1, replica_groups=mesh['dp'=16,'mp'=2] {'dp'}, dimensions={0}, use_global_device_ids=true | all-gather | bytes 626688 | tf_op jit(solution)/shard_map/all_gather | solution.py:113
  192.0 4.8 convolution_convert_fusion.3
  201.1 4.8 convolution_convert_fusion.4
  217.8 3.9 multiply_reduce_fusion.39
  227.3 4.0 reshape.597
  261.5 4.2 reshape.598
  268.0 29.7 %multiply_convert_fusion.1 = bf16[2,1024,6,64]{1,3,2,0:T(8,128)(2,1)} fusion(f32[2,1024,6,64]{1,3,2,0:T(8,128)S(1)} %copy_multiply_fusion, f32[2,6,64,64]{3,2,1,0:T(8,128)S(1)} %fusion.157, f32[6]{0:T(128)S(1)} %copy-done.159, f32[6]{0:T(128)S(1)} %copy-done.169, f32[6]{0:T(128)S(1)} %copy-done.171, f32[6]{0:T(128)S(1)} %copy-done.173, ...), kind=kOutput, calls=%fused_computation.121 | convolution fusion | flops 659816448 | bytes 8168216 | tf_op jit(solution)/shard_map/jvp(vmap(hsj,hjd->shd))/dot_general | solution.py:81
  297.6 3.7 all-to-all-start
  304.9 3.6 fusion.156
  311.6 7.5 all-gather.11.cloned.1.call-done
  319.1 35.5 %multiply_convert_fusion = (bf16[2048,1536]{1,0:T(8,128)(2,1)}, f32[2048,1536]{1,0:T(8,128)}, f32[2048,1536]{1,0:T(8,128)}) fusion(bf16[2048,768]{0,1:T(8,128)(2,1)} %all-gather.11.cloned.1.call-done, bf16[768,1536]{1,0:T(8,128)(2,1)} %all-gather.13.cloned.1.call-done), kind=kOutput, calls=%fused_computation.3 | convolution fusion | flops 5036310528 | bytes 36962304 | tf_op jit(solution)/shard_map/dot_general | solution.py:14
  354.6 30.5 %all-gather.15.cloned.1.call-done = bf16[1536,768]{0,1:T(8,128)(2,1)} async-done(((bf16[1536,48]{0,1:T(8,128)(2,1)}), bf16[1536,768]{0,1:T(8,128)(2,1)}) %all-gather.15.cloned.1.call-update) | async-done | bytes 2359312 | tf_op jit(solution)/shard_map/all_gather | solution.py:115
  385.2 9.0 convolution_convert_fusion.1
  397.4 6.3 reduce-scatter.16.cloned.1.call-done
  415.1 13.5 all-gather.17.cloned.1.call-done
  428.6 17.3 %add_convert_fusion = bf16[2048,1536]{1,0:T(8,128)(2,1)S(1)} fusion(f32[2048,1536]{1,0:T(8,128)} %get-tuple-element.153, f32[2048,1536]{1,0:T(8,128)} %get-tuple-element.200, bf16[2048,768]{0,1:T(8,128)(2,1)} %all-gather.17.cloned.1.call-done, bf16[1536,768]{0,1:T(8,128)(2,1)} %all-gather.15.cloned.1.call-done), kind=kOutput, calls=%fused_computation.2 | convolution fusion | flops 4875878400 | bytes 36962304 | tf_op jit(solution)/shard_map/dot_general | solution.py:18
  448.6 6.4 convolution_convert_fusion
  459.4 8.0 reduce-scatter.18.cloned.1.call-done
  467.4 4.5 multiply_reduce_fusion
  475.5 5.0 all_to_all.29
  486.2 5.6 fusion.15
  534.2 15.2 %multiply_reduce_fusion.32 = (f32[6]{0:T(128)S(1)}, f32[6]{0:T(128)}, f32[6]{0:T(128)}, f32[6]{0:T(128)}, f32[6]{0:T(128)}, /*index=5*/f32[6]{0:T(128)}, f32[6]{...) fusion(f32[2,1024,6,64]{1,3,2,0:T(8,128)S(1)} %copy-done.5, ...), kind=kLoop, calls=%fused_computation.107 | loop fusion | flops 25952166 | bytes 12591512 | tf_op jit(solution)/shard_map/transpose(jvp(vmap()))/reduce_sum | solution.py:85
  549.5 16.9 %broadcast_multiply_fusion.1 = (f32[2,1024,6,64]{1,3,2,0:T(8,128)}, f32[2,1024,6,64]{1,3,2,0:T(8,128)}, f32[2,1024,6,64]{1,3,2,0:T(8,128)}, f32[2,1024,6,64]{1,3...) fusion(f32[6]{0:T(128)S(1)} %copy-done.170, ...), kind=kLoop, calls=%fused_computation.168 | loop fusion | flops 11796480 | bytes 47194448 | tf_op jit(solution)/shard_map/transpose(jvp(vmap()))/mul | solution.py:85
  566.4 21.3 %broadcast_multiply_fusion = (f32[2,1024,6,64]{1,3,2,0:T(8,128)}, f32[2,1024,6,64]{1,3,2,0:T(8,128)}, f32[2,1024,6,64]{1,3,2,0:T(8,128)}, f32[2,1024,6,64]{1,3,2...) fusion(f32[6]{0:T(128)} %get-tuple-element.134, ...), kind=kLoop, calls=%fused_computation.167 | loop fusion | flops 14155776 | bytes 56631704 | tf_op jit(solution)/shard_map/transpose(jvp(vmap()))/mul | solution.py:85
  587.8 5.0 multiply_reduce_fusion.34
  592.8 4.3 fusion.143
  600.8 3.8 multiply_reduce_fusion.35
  604.7 3.9 fusion.142
  621.6 4.4 fusion.174
  626.0 4.4 fusion.173
  630.4 34.7 %pad_add_fusion = f32[2,1056,6,64]{1,3,2,0:T(8,128)} fusion(f32[2,1024,6,64]{1,3,2,0:T(8,128)} %get-tuple-element.163, f32[2,1024,6,64]{1,3,2,0:T(8,128)} %get-tuple-element.164, f32[2,1024,6,64]{1,3,2,0:T(8,128)} %get-tuple-element.165, f32[2,1024,6,64]{1,3,2,0:T(8,128)} %get-tuple-element.166, f32[2,1024,6,64]{1,3,2,0:T(8,128)} %get-tuple-element.167, ...), kind=kLoop, calls=%fused_computation.25 | loop fusion | flops 21086208 | bytes 88178688 | tf_op jit(solution)/shard_map/transpose(jvp(vmap()))/add_any | solution.py:85
  665.2 12.1 fusion.12
  684.2 4.8 convolution_bitcast_fusion.2
  691.7 5.0 convolution_bitcast_fusion.1
  699.5 4.8 convolution_bitcast_fusion
  707.0 5.2 fusion.74
  712.3 9.6 fusion.175
  721.9 9.7 fusion.172
  734.6 28.5 %multiply_reduce_fusion.33 = (f32[6]{0:T(128)S(1)}, f32[6]{0:T(128)S(1)}, f32[6]{0:T(128)S(1)}, f32[6]{0:T(128)S(1)}, f32[6]{0:T(128)S(1)}, /*index=5*/f32[6]{0:...) fusion(f32[2,1024,6,64]{1,3,2,0:T(8,128)} %copy-done.4, ...), kind=kLoop, calls=%fused_computation.108 | loop fusion | flops 27525018 | bytes 6300056 | tf_op jit(solution)/shard_map/transpose(jvp(vmap()))/reduce_sum | solution.py:85
  778.2 40.1 %all-reduce.75 = (f32[768]{0:T(1024)S(1)}, f32[768]{0:T(1024)S(1)}, f32[768]{0:T(1024)S(1)}, f32[768]{0:T(1024)S(1)}) all-reduce(f32[768]{0:T(1024)S(1)} %copy-done.126, f32[768]{0:T(1024)S(1)} %copy-done.127, f32[768]{0:T(1024)S(1)} %copy-done.124, f32[768]{0:T(1024)S(1)} %copy-done.125), channel_id=9, replica_groups=mesh['dp'=16,'mp'=2] {'dp','mp'}, use_global_device_ids=true, to_apply=%region_64.65.clone | all-reduce | flops 3072 | bytes 24576
  828.1 129.4 %reduce-scatter.30.cloned.1.call-done = f32[48,384]{1,0:T(8,128)} async-done(((f32[768,384]{1,0:T(8,128)}), f32[48,384]{1,0:T(8,128)}) %reduce-scatter.30.cloned.1.call-update) | async-done | bytes 73744
  957.5 129.2 %reduce-scatter.32.cloned.1.call-done = f32[48,384]{1,0:T(8,128)} async-done(((f32[768,384]{1,0:T(8,128)}), f32[48,384]{1,0:T(8,128)}) %reduce-scatter.32.cloned.1.call-update) | async-done | bytes 73744
  1086.7 104.5 %reduce-scatter.22.cloned.1.call-done = f32[768,24]{0,1:T(8,128)} async-done(((f32[768,768]{0,1:T(8,128)}), f32[768,24]{0,1:T(8,128)}) %reduce-scatter.22.cloned.1.call-update) | async-done | bytes 73744 | tf_op jit(solution)/shard_map/reduce_scatter | solution.py:208
  1191.2 143.0 %reduce-scatter.26.cloned.1.call-done = f32[1536,48]{0,1:T(8,128)} async-done(((f32[1536,768]{0,1:T(8,128)}), f32[1536,48]{0,1:T(8,128)}) %reduce-scatter.26.cloned.1.call-update) | async-done | bytes 294928 | tf_op jit(solution)/shard_map/reduce_scatter | solution.py:205
  1334.2 143.4 %reduce-scatter.24.cloned.1.call-done = f32[48,1536]{1,0:T(8,128)} async-done(((f32[768,1536]{1,0:T(8,128)}), f32[48,1536]{1,0:T(8,128)}) %reduce-scatter.24.cloned.1.call-update) | async-done | bytes 294928 | tf_op jit(solution)/shard_map/reduce_scatter | solution.py:204
  (658 shorter events, 204.4 us)
Async XLA Ops:
  7.2 55.0 %copy-start.202 = (s32[32]{0:T(128)S(1)}, s32[32]{0:T(128)}, u32[]{:S(2)}) copy-start(s32[32]{0:T(128)} %param.26) | copy-start | bytes 388
  7.2 55.2 %copy-start.119 = (bf16[48,384]{1,0:T(8,128)(2,1)S(1)}, bf16[48,384]{1,0:T(8,128)(2,1)}, u32[]{:S(2)}) copy-start(bf16[48,384]{1,0:T(8,128)(2,1)} %param.15) | copy-start | bytes 110596
  7.2 99.1 %copy-start.120 = (bf16[48,384]{1,0:T(8,128)(2,1)S(1)}, bf16[48,384]{1,0:T(8,128)(2,1)}, u32[]{:S(2)}) copy-start(bf16[48,384]{1,0:T(8,128)(2,1)} %param.16) | copy-start | bytes 110596
  7.3 140.3 %copy-start.121 = (bf16[48,384]{1,0:T(8,128)(2,1)S(1)}, bf16[48,384]{1,0:T(8,128)(2,1)}, u32[]{:S(2)}) copy-start(bf16[48,384]{1,0:T(8,128)(2,1)} %param.17) | copy-start | bytes 110596
  7.3 184.7 %all-gather.7.cloned.1.call-start = ((), (), s32[]{:S(2)}) async-start(), calls=%async_computation.11 | async-start | bytes 4718592 | tf_op jit(solution)/shard_map/all_gather | solution.py:129
  8.0 293.4 %all-gather.9.cloned.1.call-start = ((), (), s32[]{:S(2)}) async-start(), calls=%async_computation.12 | async-start | bytes 1216512 | tf_op jit(solution)/shard_map/all_gather | solution.py:118
  8.7 302.8 %all-gather.13.cloned.1.call-start = ((), (), s32[]{:S(2)}) async-start(), calls=%async_computation.14 | async-start | bytes 2506752 | tf_op jit(solution)/shard_map/all_gather | solution.py:114
  62.4 151.5 %copy-start.102 = (pred[2,1024]{1,0:T(4,128)(4,1)}, pred[2,1024]{1,0:T(4,128)(4,1)S(1)}, u32[]{:S(2)}) copy-start(pred[2,1024]{1,0:T(4,128)(4,1)S(1)} %get-tuple-element.190) | copy-start | bytes 6148
  62.4 204.7 %copy-start.94 = (f32[2,1024]{1,0:T(2,128)}, f32[2,1024]{1,0:T(2,128)S(1)}, u32[]{:S(2)}) copy-start(f32[2,1024]{1,0:T(2,128)S(1)} %get-tuple-element.191) | copy-start | bytes 24580
  106.4 94.7 %copy-start.75 = (bf16[768,384]{1,0:T(8,128)(2,1)}, bf16[768,384]{1,0:T(8,128)(2,1)S(1)}, u32[]{:S(2)}) copy-start(bf16[768,384]{1,0:T(8,128)(2,1)S(1)} %all_gather.45) | copy-start | bytes 1769476
  147.6 44.4 %copy-start.77 = (bf16[768,384]{1,0:T(8,128)(2,1)}, bf16[768,384]{1,0:T(8,128)(2,1)S(1)}, u32[]{:S(2)}) copy-start(bf16[768,384]{1,0:T(8,128)(2,1)S(1)} %all_gather.46) | copy-start | bytes 1769476
  191.8 20.5 %copy-start.109 = (s32[2,1024]{1,0:T(2,128)}, s32[2,1024]{1,0:T(2,128)S(1)}, u32[]{:S(2)}) copy-start(s32[2,1024]{1,0:T(2,128)S(1)} %and_select_fusion) | copy-start | bytes 24580
  192.0 20.3 %copy-start.128 = (f32[2,64]{1,0:T(2,128)}, f32[2,64]{1,0:T(2,128)S(1)}, u32[]{:S(2)}) copy-start(f32[2,64]{1,0:T(2,128)S(1)} %convert_reduce_fusion.1) | copy-start | bytes 1540
  216.3 38.5 %copy-start = (f32[2,6,64,1024]{3,2,1,0:T(8,128)}, f32[2,6,64,1024]{3,2,1,0:T(8,128)S(1)}, u32[]{:S(2)}) copy-start(f32[2,6,64,1024]{3,2,1,0:T(8,128)S(1)} %get-tuple-element.195) | copy-start | bytes 9437188
  267.1 30.5 %copy-start.4 = (f32[2,1024,6,64]{1,3,2,0:T(8,128)}, f32[2,1024,6,64]{1,3,2,0:T(8,128)S(1)}, u32[]{:S(2)}) copy-start(f32[2,1024,6,64]{1,3,2,0:T(8,128)S(1)} %copy_multiply_fusion) | copy-start | bytes 9437188
  297.6 6.2 all-to-all-start
  301.3 17.8 %all-gather.11.cloned.1.call-start = ((), (), s32[]{:S(2)}) async-start(), calls=%async_computation.13 | async-start | bytes 4718592 | tf_op jit(solution)/shard_map/all_gather | solution.py:155
  310.9 74.2 %all-gather.15.cloned.1.call-start = ((), (), s32[]{:S(2)}) async-start(), calls=%async_computation.15 | async-start | bytes 2506752 | tf_op jit(solution)/shard_map/all_gather | solution.py:115
  311.5 92.2 %reduce-scatter.16.cloned.1.call-start = ((), (), s32[]{:S(2)}) async-start(), calls=%async_computation.16 | async-start | bytes 4718592 | tf_op jit(solution)/shard_map/reduce_scatter | solution.py:159
  394.2 34.4 %all-gather.17.cloned.1.call-start = ((), (), s32[]{:S(2)}) async-start(), calls=%async_computation.17 | async-start | bytes 4718592 | tf_op jit(solution)/shard_map/all_gather | solution.py:165
  415.1 52.3 %reduce-scatter.18.cloned.1.call-start = ((), (), s32[]{:S(2)}) async-start(), calls=%async_computation.18 | async-start | bytes 4718592 | tf_op jit(solution)/shard_map/reduce_scatter | solution.py:177
  428.6 20.0 %copy-start.204 = (bf16[768,1536]{1,0:T(8,128)(2,1)S(1)}, bf16[768,1536]{1,0:T(8,128)(2,1)}, u32[]{:S(2)}) copy-start(bf16[768,1536]{1,0:T(8,128)(2,1)} %all-gather.13.cloned.1.call-done) | copy-start | bytes 7077892
  455.1 366.3 %reduce-scatter.20.cloned.1.call-start = ((), (), s32[]{:S(2)}) async-start(), calls=%async_computation.19 | async-start | bytes 4718592 | tf_op jit(solution)/shard_map/reduce_scatter | solution.py:194
  566.4 21.3 %copy-start.104 = (pred[2,1024]{1,0:T(4,128)(4,1)S(1)}, pred[2,1024]{1,0:T(4,128)(4,1)}, u32[]{:S(2)}) copy-start(pred[2,1024]{1,0:T(4,128)(4,1)} %copy-done.102) | copy-start | bytes 6148
  684.1 144.0 %reduce-scatter.28.cloned.1.call-start = ((), (), s32[]{:S(2)}) async-start(), calls=%async_computation.23 | async-start | bytes 1253376
  691.7 265.9 %reduce-scatter.30.cloned.1.call-start = ((), (), s32[]{:S(2)}) async-start(), calls=%async_computation.24 | async-start | bytes 1253376
  699.4 387.3 %reduce-scatter.32.cloned.1.call-start = ((), (), s32[]{:S(2)}) async-start(), calls=%async_computation.25 | async-start | bytes 1253376
  706.9 484.3 %reduce-scatter.22.cloned.1.call-start = ((), (), s32[]{:S(2)}) async-start(), calls=%async_computation.20 | async-start | bytes 2433024 | tf_op jit(solution)/shard_map/reduce_scatter | solution.py:208
  712.2 622.0 %reduce-scatter.26.cloned.1.call-start = ((), (), s32[]{:S(2)}) async-start(), calls=%async_computation.22 | async-start | bytes 5013504 | tf_op jit(solution)/shard_map/reduce_scatter | solution.py:205
  721.9 755.7 %reduce-scatter.24.cloned.1.call-start = ((), (), s32[]{:S(2)}) async-start(), calls=%async_computation.21 | async-start | bytes 5013504 | tf_op jit(solution)/shard_map/reduce_scatter | solution.py:204
  734.5 28.7 %copy-start.133 = (f32[6]{0:T(128)S(1)}, f32[6]{0:T(128)}, u32[]{:S(2)}) copy-start(f32[6]{0:T(128)} %get-tuple-element.85) | copy-start | bytes 76
  734.5 28.7 %copy-start.134 = (f32[6]{0:T(128)S(1)}, f32[6]{0:T(128)}, u32[]{:S(2)}) copy-start(f32[6]{0:T(128)} %get-tuple-element.86) | copy-start | bytes 76
  734.5 28.7 %copy-start.135 = (f32[6]{0:T(128)S(1)}, f32[6]{0:T(128)}, u32[]{:S(2)}) copy-start(f32[6]{0:T(128)} %get-tuple-element.87) | copy-start | bytes 76
  734.5 28.7 %copy-start.136 = (f32[6]{0:T(128)S(1)}, f32[6]{0:T(128)}, u32[]{:S(2)}) copy-start(f32[6]{0:T(128)} %get-tuple-element.88) | copy-start | bytes 76
  734.5 28.7 %copy-start.137 = (f32[6]{0:T(128)S(1)}, f32[6]{0:T(128)}, u32[]{:S(2)}) copy-start(f32[6]{0:T(128)} %get-tuple-element.89) | copy-start | bytes 76
  734.5 28.7 %copy-start.138 = (f32[6]{0:T(128)S(1)}, f32[6]{0:T(128)}, u32[]{:S(2)}) copy-start(f32[6]{0:T(128)} %get-tuple-element.90) | copy-start | bytes 76
  734.5 28.7 %copy-start.139 = (f32[6]{0:T(128)S(1)}, f32[6]{0:T(128)}, u32[]{:S(2)}) copy-start(f32[6]{0:T(128)} %get-tuple-element.91) | copy-start | bytes 76
  734.5 28.7 %copy-start.140 = (f32[6]{0:T(128)S(1)}, f32[6]{0:T(128)}, u32[]{:S(2)}) copy-start(f32[6]{0:T(128)} %get-tuple-element.92) | copy-start | bytes 76
  734.6 28.7 %copy-start.141 = (f32[6]{0:T(128)S(1)}, f32[6]{0:T(128)}, u32[]{:S(2)}) copy-start(f32[6]{0:T(128)} %get-tuple-element.93) | copy-start | bytes 76
  734.6 28.7 %copy-start.142 = (f32[6]{0:T(128)S(1)}, f32[6]{0:T(128)}, u32[]{:S(2)}) copy-start(f32[6]{0:T(128)} %get-tuple-element.94) | copy-start | bytes 76
  734.6 28.7 %copy-start.143 = (f32[6]{0:T(128)S(1)}, f32[6]{0:T(128)}, u32[]{:S(2)}) copy-start(f32[6]{0:T(128)} %get-tuple-element.95) | copy-start | bytes 76
  734.6 28.7 %copy-start.144 = (f32[6]{0:T(128)S(1)}, f32[6]{0:T(128)}, u32[]{:S(2)}) copy-start(f32[6]{0:T(128)} %get-tuple-element.96) | copy-start | bytes 76
  734.6 28.7 %copy-start.145 = (f32[6]{0:T(128)S(1)}, f32[6]{0:T(128)}, u32[]{:S(2)}) copy-start(f32[6]{0:T(128)} %get-tuple-element.97) | copy-start | bytes 76
  734.6 28.7 %copy-start.146 = (f32[6]{0:T(128)S(1)}, f32[6]{0:T(128)}, u32[]{:S(2)}) copy-start(f32[6]{0:T(128)} %get-tuple-element.98) | copy-start | bytes 76
  763.3 3.8 collective-permute-start
  767.2 3.8 collective-permute-start.1
  771.1 4.5 collective-permute-start.2
  775.7 45.0 %collective-permute-start.3 = (f32[6,33]{0,1:T(8,128)S(1)}, f32[6,33]{0,1:T(8,128)S(1)}, u32[]{:S(2)}, u32[]{:S(2)}) collective-permute-start(f32[6,33]{0,1:T(8,128)S(1)} %add.381), channel_id=1, source_target_pairs={{0,16},{2,18},{4,20},{6,22},{8,24},{10,26},{12,28},{14,30},{16,0},... | collective-permute-start | bytes 2384 | tf_op jit(solution)/shard_map/ppermute | solution.py:217
  (189 other events, 885.0 us)
Sparse Core Ops, SparseCore 0:
  9.6 14.8 all-gather.6
  27.4 56.5 all-gather.8
  86.7 69.0 all-gather.12
  311.0 8.0 all-gather.10
  321.7 63.3 all-gather.14
  394.3 9.3 reduce-scatter.15
  415.2 13.3 all-gather.16
  455.2 12.1 reduce-scatter.17
  684.2 12.2 reduce-scatter.19
  701.7 126.4 reduce-scatter.27
  833.5 124.0 reduce-scatter.29
  962.7 123.9 reduce-scatter.31
  1092.6 98.5 reduce-scatter.21
  1196.8 137.3 reduce-scatter.25
  1339.8 137.7 reduce-scatter.23
